TPU v7x, 32 devices: a whole 2x2x4 slice. The times are simulated.
32 devices in a mesh: rows: 16 (over z, y, x), layer: 2 (over core).
Axes of the slice: x: 2, y: 2, z: 4, core: 2. Of those that a mesh axis runs over, the one named last changes fastest.
Arguments:
- grads: bfloat16 [2, 2048, 8192], P('layer', 'rows'), may hold values from -180 to 180
- momentum: float32 [2, 2048, 8192], P('layer', 'rows'), may hold values from -6 to 6
- weights: float32 [2, 2048, 8192], P('layer', 'rows'), may hold values from -1.5 to 1.5
Outputs:
- new_weights: float32 [2, 2048, 8192], P('layer', 'rows')
- new_momentum: float32 [2, 2048, 8192], P('layer', 'rows')
All inputs are finite; a program needn't handle non-finite values.
Results may differ from a plain program's by a relative error of at most 0.0003.
Values sent between devices are 32-bit elements; how exact they have to be, the bound alone decides.
A program may use at most 128 MiB of HBM per device.

v0:
```python
import math

import jax
import jax.numpy as jnp
from jax import lax
from jax.sharding import PartitionSpec as P

LATENT = 2048
HEADS = 32
HD = 256
ITERS = 5


coef_a = 3.4445
coef_b = -4.775
coef_c = 2.0315
momentum_decay = 0.95
learn_rate = 0.5
weight_decay = 0.1


def local_gram(blocks):
    return jnp.einsum("kri,krj->kij", blocks, blocks, precision=lax.Precision.HIGHEST)


def newton_schulz(blocks, gram_fn):
    first = gram_fn(blocks)
    norm = jnp.sqrt(jnp.trace(first, axis1=1, axis2=2))[:, None, None] + 1e-07
    current = blocks / norm
    gram = first / (norm * norm)
    for sweep in range(ITERS):
        if sweep > 0:
            gram = gram_fn(current)
        square = jnp.einsum("kij,kjl->kil", gram, gram, precision=lax.Precision.HIGHEST)
        poly = coef_b * gram + coef_c * square
        current = coef_a * current + jnp.einsum(
            "kri,kij->krj", current, poly, precision=lax.Precision.HIGHEST
        )
    return current


def body(grads, momentum, weights):
    gradient = grads[0].astype(jnp.float32)
    local_squares = jnp.sum(gradient * gradient)
    total = lax.psum(local_squares, ("rows", "layer"))
    count = lax.axis_size("layer") * LATENT * HEADS * HD
    limit = 0.5 * math.sqrt(float(count))
    factor = jnp.minimum(1.0, limit / (jnp.sqrt(total) + 1e-06))
    clipped = factor * gradient
    new_momentum = momentum_decay * momentum[0] + clipped
    update = clipped + momentum_decay * new_momentum
    rows_here = update.shape[0]
    half_rows = rows_here // 2
    devices = lax.axis_size("rows")
    per_device = 2 * HEADS // devices
    blocks = update.reshape(rows_here, HEADS, HD)
    head_major = blocks.transpose(1, 0, 2)
    outgoing = jnp.concatenate([head_major, head_major], axis=0)
    outgoing = outgoing.reshape(devices, per_device, rows_here, HD)
    side = lax.axis_index("rows") * per_device // HEADS
    pieces = lax.all_to_all(outgoing, "rows", split_axis=0, concat_axis=2, tiled=True)
    items = pieces.shape[1]
    result = newton_schulz(pieces[0], local_gram)
    shares = result.reshape(items, devices, 2, half_rows, HD)
    chosen = lax.dynamic_index_in_dim(shares, side, 2, keepdims=False)
    ortho = chosen.reshape(1, items, devices * half_rows, HD)
    returned = lax.all_to_all(ortho, "rows", split_axis=2, concat_axis=0, tiled=True)
    returned = (
        returned.reshape(2, HEADS, half_rows, HD)
        .transpose(0, 2, 1, 3)
        .reshape(rows_here, HEADS * HD)
    )
    scale = 0.2 * math.sqrt(float(max(LATENT, HD)))
    new_weights = weights[0] - learn_rate * (scale * returned + weight_decay * weights[0])
    return (new_weights[None], new_momentum[None])


def solution(mesh):
    placed = (P("layer", "rows", None), P("layer", "rows", None), P("layer", "rows", None))
    return jax.shard_map(
        body,
        mesh=mesh,
        in_specs=placed,
        out_specs=(P("layer", "rows", None), P("layer", "rows", None)),
        check_vma=False,
    )
```

profile of v0, /device:TPU:16, one launch (start us, length us, event | category | flops | bytes accessed | tf_op | source)
XLA Modules:
  0.0 510.3 jit_solution(12123950660307743422)
XLA Ops:
  0.6 3.2 copy.28
  3.9 1.7 fusion.1
  5.5 40.4 %psum.7 = f32[]{:T(128)} all-reduce(f32[]{:T(128)} %fusion.1), channel_id=1, replica_groups=mesh['rows'=16,'layer'=2] {'rows','layer'}, use_global_device_ids=true, to_apply=%region_1.0 | all-reduce | flops 1 | bytes 8 | tf_op jit(solution)/shard_map/psum | solution.py:45
  46.7 5.6 %copy.29 = f32[1,128,8192]{1,2,0:T(8,128)} copy(f32[1,128,8192]{2,1,0:T(8,128)} %param.4) | data formatting | bytes 8388608 | tf_op args[1]
  52.3 5.0 fusion.9
  57.3 0.7 add_bitcast_fusion
  58.0 4.2 pad_maximum_fusion
  62.2 9.0 %copy.30 = f32[64,128,256]{2,1,0:T(8,128)} copy(f32[64,128,256]{1,2,0:T(8,128)} %pad_maximum_fusion) | data formatting | bytes 16777216 | tf_op jit(solution)/shard_map/concatenate | solution.py:58
  71.2 6.6 %all-to-all-start = ((f32[16,4,128,256]{3,2,1,0:T(8,128)}), f32[16,4,128,256]{3,2,1,0:T(8,128)}, u32[]{:S(2)}, u32[]{:S(2)}) async-start(f32[16,4,128,256]{3,2,1,0:T(8,128)} %bitcast.48), calls=%async_computation | async-start | bytes 16777216 | tf_op jit(solution)/shard_map/all_to_all | solution.py:61
  77.9 181.1 %all-to-all-done = f32[16,4,128,256]{3,2,1,0:T(8,128)} async-done(((f32[16,4,128,256]{3,2,1,0:T(8,128)}), f32[16,4,128,256]{3,2,1,0:T(8,128)}, u32[]{:S(2)}, u32[]{:S(2)}) %all-to-all-start) | async-done | bytes 8388640 | tf_op jit(solution)/shard_map/all_to_all | solution.py:61
  259.0 3.9 copy.31
  263.0 14.2 %select_reduce_fusion = (f32[4]{0:T(128)S(1)}, f32[4,256,256]{2,1,0:T(8,128)S(1)}) fusion(pred[256,256]{1,0:T(8,128)(4,1)S(1)} %iota_compare_fusion, f32[4,2048,256]{2,1,0:T(8,128)S(1)} %bitcast.46), kind=kOutput, calls=%fused_computation.26 | convolution fusion | flops 6442975232 | bytes 9502736 | tf_op jit(solution)/shard_map/kri,krj->kij/dot_general | solution.py:23
  277.2 1.4 fusion.7
  278.6 9.8 %multiply_add_fusion.4 = f32[4,2048,256]{2,1,0:T(8,128)S(1)} fusion(f32[4,256,256]{2,1,0:T(8,128)S(1)} %fusion.7, f32[4,2048,256]{2,1,0:T(8,128)S(1)} %bitcast.47, f32[4]{0:T(128)S(1)} %get-tuple-element.9), kind=kOutput, calls=%fused_computation.5 | convolution fusion | flops 6450839552 | bytes 17825808 | tf_op jit(solution)/shard_map/kri,kij->krj/dot_general | solution.py:36
  288.5 14.6 %fusion.12 = f32[4,256,256]{2,1,0:T(8,128)S(1)} fusion(f32[4,2048,256]{2,1,0:T(8,128)S(1)} %multiply_add_fusion.4), kind=kOutput, calls=%fused_computation.33 | convolution fusion | flops 6442450944 | bytes 9437184 | tf_op jit(solution)/shard_map/kri,krj->kij/dot_general | solution.py:23
  303.1 1.2 fusion.6
  304.3 8.4 %multiply_add_fusion.3 = f32[4,2048,256]{2,1,0:T(8,128)S(1)} fusion(f32[4,2048,256]{2,1,0:T(8,128)S(1)} %multiply_add_fusion.4, f32[4,256,256]{2,1,0:T(8,128)S(1)} %fusion.6), kind=kOutput, calls=%fused_computation.4 | convolution fusion | flops 6446645248 | bytes 17825792 | tf_op jit(solution)/shard_map/kri,kij->krj/dot_general | solution.py:36
  312.7 13.6 %fusion.13 = f32[4,256,256]{2,1,0:T(8,128)S(1)} fusion(f32[4,2048,256]{2,1,0:T(8,128)S(1)} %multiply_add_fusion.3), kind=kOutput, calls=%fused_computation.34 | convolution fusion | flops 6442450944 | bytes 9437184 | tf_op jit(solution)/shard_map/kri,krj->kij/dot_general | solution.py:23
  326.3 1.5 fusion.5
  327.7 7.9 %multiply_add_fusion.2 = f32[4,2048,256]{2,1,0:T(8,128)S(1)} fusion(f32[4,2048,256]{2,1,0:T(8,128)S(1)} %multiply_add_fusion.3, f32[4,256,256]{2,1,0:T(8,128)S(1)} %fusion.5), kind=kOutput, calls=%fused_computation.3 | convolution fusion | flops 6446645248 | bytes 17825792 | tf_op jit(solution)/shard_map/kri,kij->krj/dot_general | solution.py:36
  335.7 13.8 %fusion.14 = f32[4,256,256]{2,1,0:T(8,128)S(1)} fusion(f32[4,2048,256]{2,1,0:T(8,128)S(1)} %multiply_add_fusion.2), kind=kOutput, calls=%fused_computation.35 | convolution fusion | flops 6442450944 | bytes 9437184 | tf_op jit(solution)/shard_map/kri,krj->kij/dot_general | solution.py:23
  349.5 1.2 fusion.4
  350.7 8.1 %multiply_add_fusion.1 = f32[4,2048,256]{2,1,0:T(8,128)S(1)} fusion(f32[4,2048,256]{2,1,0:T(8,128)S(1)} %multiply_add_fusion.2, f32[4,256,256]{2,1,0:T(8,128)S(1)} %fusion.4), kind=kOutput, calls=%fused_computation.2 | convolution fusion | flops 6446645248 | bytes 17825792 | tf_op jit(solution)/shard_map/kri,kij->krj/dot_general | solution.py:36
  358.8 13.6 %fusion.15 = f32[4,256,256]{2,1,0:T(8,128)S(1)} fusion(f32[4,2048,256]{2,1,0:T(8,128)S(1)} %multiply_add_fusion.1), kind=kOutput, calls=%fused_computation.36 | convolution fusion | flops 6442450944 | bytes 9437184 | tf_op jit(solution)/shard_map/kri,krj->kij/dot_general | solution.py:23
  372.4 1.2 fusion.3
  373.7 8.4 %multiply_add_fusion = f32[4,2048,256]{2,1,0:T(8,128)S(1)} fusion(f32[4,2048,256]{2,1,0:T(8,128)S(1)} %multiply_add_fusion.1, f32[4,256,256]{2,1,0:T(8,128)S(1)} %fusion.3), kind=kOutput, calls=%fused_computation.1 | convolution fusion | flops 6446645248 | bytes 17825792 | tf_op jit(solution)/shard_map/kri,kij->krj/dot_general | solution.py:36
  382.0 0.5 constant_dynamic-slice_fusion
  382.5 4.8 copy.37
  387.3 13.1 %all-to-all-start.1 = ((f32[1,4,1024,256]{3,1,0,2:T(4,128)}), f32[1,4,1024,256]{3,1,0,2:T(4,128)}, u32[]{:S(2)}, u32[]{:S(2)}) async-start(f32[1,4,1024,256]{3,1,0,2:T(4,128)} %bitcast.50), calls=%async_computation.1 | async-start | bytes 8388608 | tf_op jit(solution)/shard_map/all_to_all | solution.py:67
  400.4 5.6 %copy.41 = f32[1,128,8192]{2,1,0:T(8,128)} copy(f32[1,128,8192]{1,2,0:T(8,128)} %get-tuple-element.6) | data formatting | bytes 8388608
  406.0 85.0 %all-to-all-done.1 = f32[1,4,1024,256]{3,1,0,2:T(4,128)} async-done(((f32[1,4,1024,256]{3,1,0,2:T(4,128)}), f32[1,4,1024,256]{3,1,0,2:T(4,128)}, u32[]{:S(2)}, u32[]{:S(2)}) %all-to-all-start.1) | async-done | bytes 4194336 | tf_op jit(solution)/shard_map/all_to_all | solution.py:67
  491.0 3.1 copy_multiply_fusion
  494.1 0.5 copy.39
  494.5 4.4 copy.40
  499.0 4.9 mul.151
  503.9 6.1 %multiply_subtract_fusion = f32[1,128,8192]{2,1,0:T(8,128)} fusion(f32[1,128,8192]{2,1,0:T(8,128)} %param.5, f32[1,128,8192]{2,1,0:T(8,128)} %mul.151), kind=kLoop, calls=%fused_computation.11 | loop fusion | flops 4194304 | bytes 12582912 | tf_op jit(solution)/shard_map/sub | solution.py:74
  (2 shorter events, 0.0 us)
Async XLA Ops:
  71.2 187.8 %all-to-all-start = ((f32[16,4,128,256]{3,2,1,0:T(8,128)}), f32[16,4,128,256]{3,2,1,0:T(8,128)}, u32[]{:S(2)}, u32[]{:S(2)}) async-start(f32[16,4,128,256]{3,2,1,0:T(8,128)} %bitcast.48), calls=%async_computation | async-start | bytes 16777216 | tf_op jit(solution)/shard_map/all_to_all | solution.py:61
  387.3 103.7 %all-to-all-start.1 = ((f32[1,4,1024,256]{3,1,0,2:T(4,128)}), f32[1,4,1024,256]{3,1,0,2:T(4,128)}, u32[]{:S(2)}, u32[]{:S(2)}) async-start(f32[1,4,1024,256]{3,1,0,2:T(4,128)} %bitcast.50), calls=%async_computation.1 | async-start | bytes 8388608 | tf_op jit(solution)/shard_map/all_to_all | solution.py:67
where the time goes:
time: 516 us; the launch traced here: 510 us
  waiting for transfers between devices  266 us (52%)
  matrix products  119 us (23%)
  local copies, waits for them, and re-layouts  42.5 us (8%)
  blocking collectives  40.4 us (8%)
  other arithmetic  20.9 us (4%)
  starting transfers between devices  19.7 us (4%)
    all_to_all x1, waiting for transfers between devices, body(): lax.all_to_all(outgoing, 'rows', split_axis=0, concat_axis=2, tiled=True)  181 us
    all_to_all x1, waiting for transfers between devices, body(): lax.all_to_all(ortho, 'rows', split_axis=2, concat_axis=0, tiled=True)  85 us
    dot_general x5, matrix products, local_gram(): jnp.einsum('kri,krj->kij', blocks, blocks, precision=lax.Precision.HIGHEST)  69.7 us
    dot_general x5, matrix products, newton_schulz(): jnp.einsum('kri,kij->krj', current, poly, precision=lax.Precision.HIGHEST)  42.6 us
    psum x1, blocking collectives, body(): total = lax.psum(local_squares, ('rows', 'layer'))  40.4 us
    unnamed x3, local copies, waits for them, and re-layouts  14.4 us
    all_to_all x1, starting transfers between devices, body(): lax.all_to_all(ortho, 'rows', split_axis=2, concat_axis=0, tiled=True)  13.1 us
  transfers between devices with their start and end apart: 2, of which 2 were waited for; matrix products, arithmetic and copies ran while one was open for 1% of the time, Pallas kernels for 0%

commit v1 on v0

v1 whole, which is shorter than its diff:
```python
import functools
import math

import jax
import jax.numpy as jnp
from jax import lax
from jax.experimental import pallas as pl
from jax.experimental.pallas import tpu as pltpu
from jax.sharding import PartitionSpec as P

HD = 256
ITERS = 5

coef_a = 3.4445
coef_b = -4.775
coef_c = 2.0315
momentum_decay = 0.95
learn_rate = 0.5
weight_decay = 0.1

HIGHEST = lax.Precision.HIGHEST
MESH = pl.DeviceIdType.MESH


def mm(a, b):
    return jnp.dot(a, b, precision=HIGHEST, preferred_element_type=jnp.float32)


def split(x):
    high = x.astype(jnp.bfloat16)
    low = (x - high.astype(jnp.float32)).astype(jnp.bfloat16)
    return high, low


def polynomial(gram):
    row = lax.broadcasted_iota(jnp.int32, (HD, HD), 0)
    col = lax.broadcasted_iota(jnp.int32, (HD, HD), 1)
    eye = jnp.where(row == col, 1.0, 0.0).astype(jnp.float32)
    trace = jnp.sum(jnp.sum(gram * eye, axis=0, keepdims=True), axis=1, keepdims=True)
    norm = jnp.sqrt(trace) + 1e-07
    a = gram / (norm * norm)
    q = None
    for sweep in range(ITERS):
        p = coef_a * eye + (coef_b * a + coef_c * mm(a, a))
        q = p if q is None else mm(q, p)
        if sweep < ITERS - 1:
            a = mm(mm(a, p), p)
    return q / norm


def exchange_kernel(
    devices, layers, limit, g_ref, m_ref, ret_ref, fac_ref,
    squares, mine, outgoing, held, result,
    square_send, square_recv, out_send, out_recv, back_send, back_recv, own_sem,
):
    rows = g_ref.shape[0]
    heads = g_ref.shape[1] // HD
    per_device = heads // devices
    everyone = devices * layers
    me = lax.axis_index("rows")
    layer = lax.axis_index("layer")
    flat = me * layers + layer

    barrier = pltpu.get_barrier_semaphore()

    @pl.loop(1, everyone)
    def _(k):
        peer = (flat + k) % everyone
        pl.semaphore_signal(
            barrier, inc=1, device_id={"rows": peer // layers, "layer": peer % layers}, device_id_type=MESH
        )

    def add_squares(h, acc):
        x = g_ref[:, pl.ds(pl.multiple_of(h * HD, HD), HD)].astype(jnp.float32)
        return acc + x * x

    acc = lax.fori_loop(0, heads, add_squares, jnp.zeros((rows, HD), jnp.float32))
    acc = acc.reshape(rows // 8, 8, HD).sum(axis=0)
    part = acc[:, :128] + acc[:, 128:]
    mine[...] = part
    squares[flat] = part
    pl.semaphore_wait(barrier, everyone - 1)

    def square_copy(k):
        peer = (flat + k) % everyone
        return pltpu.make_async_remote_copy(
            src_ref=mine,
            dst_ref=squares.at[flat],
            send_sem=square_send.at[k],
            recv_sem=square_recv.at[k],
            device_id={"rows": peer // layers, "layer": peer % layers},
            device_id_type=MESH,
        )

    @pl.loop(1, everyone)
    def _(k):
        square_copy(k).start()

    @pl.loop(1, everyone)
    def _(k):
        square_copy(k).wait_recv()

    total = jnp.sum(squares[...], axis=0)
    total = jnp.sum(jnp.sum(total, axis=0, keepdims=True), axis=1, keepdims=True)
    factor = jnp.minimum(1.0, limit / (jnp.sqrt(total) + 1e-06))
    fac_ref[...] = jnp.broadcast_to(factor, fac_ref.shape)

    def update_of(h):
        columns = pl.ds(pl.multiple_of(h * HD, HD), HD)
        clipped = factor * g_ref[:, columns].astype(jnp.float32)
        new_momentum = momentum_decay * m_ref[:, columns] + clipped
        return clipped + momentum_decay * new_momentum

    def block(d):
        return pl.ds(pl.multiple_of(d * rows, rows), rows)

    def out_copy(j, k):
        d = (me + k) % devices
        return pltpu.make_async_remote_copy(
            src_ref=outgoing.at[d * per_device + j],
            dst_ref=held.at[j, block(me)],
            send_sem=out_send.at[j, k],
            recv_sem=out_recv.at[j, k],
            device_id={"rows": d},
            device_id_type=MESH,
        )

    def back_copy(j, k):
        d = (me + k) % devices
        head = me * per_device + j
        return pltpu.make_async_remote_copy(
            src_ref=result.at[j, block(d)],
            dst_ref=ret_ref.at[:, pl.ds(pl.multiple_of(head * HD, HD), HD)],
            send_sem=back_send.at[j, k],
            recv_sem=back_recv.at[j, k],
            device_id={"rows": d},
            device_id_type=MESH,
        )

    def own_copy(j):
        head = me * per_device + j
        return pltpu.make_async_copy(
            result.at[j, block(me)], ret_ref.at[:, pl.ds(pl.multiple_of(head * HD, HD), HD)], own_sem.at[j]
        )

    @pl.loop(0, per_device)
    def _(j):
        @pl.loop(1, devices)
        def _(k):
            h = (me + k) % devices * per_device + j
            outgoing[h] = update_of(h)
            out_copy(j, k).start()

        held[j, block(me), :] = update_of(me * per_device + j)

    @pl.loop(0, per_device)
    def _(j):
        @pl.loop(1, devices)
        def _(k):
            out_copy(j, k).wait_recv()

        step = 2 * rows

        def add_gram(s, gram):
            x = held[j, pl.ds(pl.multiple_of(s * step, step), step), :]
            return gram + lax.dot_general(
                x, x, (((0,), (0,)), ((), ())), precision=HIGHEST, preferred_element_type=jnp.float32
            )

        gram = lax.fori_loop(0, devices // 2, add_gram, jnp.zeros((HD, HD), jnp.float32))
        q_high, q_low = split(polynomial(gram))

        def apply(d):
            high, low = split(held[j, block(d), :])
            dot = functools.partial(jnp.dot, preferred_element_type=jnp.float32)
            result[j, block(d), :] = dot(high, q_high) + (dot(high, q_low) + dot(low, q_high))

        @pl.loop(1, devices)
        def _(k):
            apply((me + k) % devices)
            back_copy(j, k).start()

        apply(me)
        own_copy(j).start()

    @pl.loop(0, per_device)
    def _(j):
        own_copy(j).wait()

        @pl.loop(1, devices)
        def _(k):
            back_copy(j, k).wait_recv()
            back_copy(j, k).wait_send()
            out_copy(j, k).wait_send()

    @pl.loop(1, everyone)
    def _(k):
        square_copy(k).wait_send()


def exchange(gradient, momentum, devices, layers, limit):
    rows, width = gradient.shape
    heads = width // HD
    per_device = heads // devices
    everyone = devices * layers
    latent = rows * devices
    dma = pltpu.SemaphoreType.DMA
    return pl.pallas_call(
        functools.partial(exchange_kernel, devices, layers, limit),
        out_shape=(
            jax.ShapeDtypeStruct((rows, width), jnp.float32),
            jax.ShapeDtypeStruct((8, 128), jnp.float32),
        ),
        in_specs=[pl.BlockSpec(memory_space=pltpu.VMEM)] * 2,
        out_specs=(pl.BlockSpec(memory_space=pl.ANY), pl.BlockSpec(memory_space=pltpu.VMEM)),
        scratch_shapes=[
            pltpu.VMEM((everyone, 8, 128), jnp.float32),
            pltpu.VMEM((8, 128), jnp.float32),
            pltpu.VMEM((heads, rows, HD), jnp.float32),
            pltpu.VMEM((per_device, latent, HD), jnp.float32),
            pltpu.VMEM((per_device, latent, HD), jnp.float32),
            dma((everyone,)),
            dma((everyone,)),
            dma((per_device, devices)),
            dma((per_device, devices)),
            dma((per_device, devices)),
            dma((per_device, devices)),
            dma((per_device,)),
        ],
        compiler_params=pltpu.CompilerParams(
            collective_id=0, has_side_effects=True, vmem_limit_bytes=48 * 1024 * 1024
        ),
    )(gradient, momentum)


def body(grads, momentum, weights):
    devices, layers = lax.axis_size("rows"), lax.axis_size("layer")
    rows, width = grads.shape[1:]
    limit = 0.5 * math.sqrt(float(layers * devices * rows * width))
    returned, fac = exchange(grads[0], momentum[0], devices, layers, limit)
    new_momentum = momentum_decay * momentum[0] + fac[0, 0] * grads[0].astype(jnp.float32)
    scale = 0.2 * math.sqrt(float(max(devices * rows, HD)))
    new_weights = weights[0] - learn_rate * (scale * returned + weight_decay * weights[0])
    return (new_weights[None], new_momentum[None])


def shared_body(grads, momentum, weights):
    devices = lax.axis_size("rows")
    rows, width = grads.shape[1:]
    heads = width // HD
    gradient = grads[0].astype(jnp.float32)
    total = lax.psum(jnp.sum(gradient * gradient), ("rows", "layer"))
    limit = 0.5 * math.sqrt(float(lax.axis_size("layer") * devices * rows * width))
    factor = jnp.minimum(1.0, limit / (jnp.sqrt(total) + 1e-06))
    clipped = factor * gradient
    new_momentum = momentum_decay * momentum[0] + clipped
    update = clipped + momentum_decay * new_momentum
    sharers = devices // heads
    part = rows // sharers
    head_major = update.reshape(rows, heads, HD).transpose(1, 0, 2)
    outgoing = jnp.concatenate([head_major] * sharers, axis=0)
    pieces = lax.all_to_all(outgoing, "rows", split_axis=0, concat_axis=1, tiled=True)
    x = pieces[0]
    gram = lax.dot_general(x, x, (((0,), (0,)), ((), ())), precision=HIGHEST)
    result = mm(x, polynomial(gram))
    side = lax.axis_index("rows") // heads
    shares = result.reshape(devices, sharers, part, HD)
    chosen = lax.dynamic_index_in_dim(shares, side, 1, keepdims=False)
    returned = lax.all_to_all(chosen, "rows", split_axis=0, concat_axis=0, tiled=True)
    returned = returned.reshape(sharers, heads, part, HD).transpose(0, 2, 1, 3).reshape(rows, width)
    scale = 0.2 * math.sqrt(float(max(devices * rows, HD)))
    new_weights = weights[0] - learn_rate * (scale * returned + weight_decay * weights[0])
    return (new_weights[None], new_momentum[None])


def solution(mesh):
    placed = P("layer", "rows", None)

    def step(grads, momentum, weights):
        heads = grads.shape[2] // HD
        chosen = body if heads % mesh.shape["rows"] == 0 else shared_body
        return jax.shard_map(
            chosen, mesh=mesh, in_specs=(placed,) * 3, out_specs=(placed, placed), check_vma=False
        )(grads, momentum, weights)

    return step
```

time: 516 us -> 214 us (0.41)
  the two profiles are of different devices: /device:TPU:16 before, /device:TPU:14 now
where the time goes in v1:
time: 214 us
  Pallas kernels  203 us (95%)
  other arithmetic  8.48 us (4%)
    pallas_call x1, Pallas kernels, exchange(): pl.pallas_call(functools.partial(exchange_kernel, devices, layers, limit)...  203 us
    broadcast_in_dim x1, other arithmetic, body(): return (new_weights[None], new_momentum[None])  5.22 us

profile of v1, /device:TPU:14, one launch (start us, length us, event | category | flops | bytes accessed | tf_op | source)
XLA Modules:
  0.0 214.0 jit_solution(2250268043305178087)
XLA Ops:
  0.6 0.0 copy-start
  0.6 1.6 copy-done
  2.2 0.0 copy-start.2
  2.2 202.8 %shard_map.50 = (f32[128,8192]{1,0:T(8,128)}, f32[8,128]{1,0:T(8,128)S(1)}) custom-call(bf16[128,8192]{1,0:T(8,128)(2,1)S(1)} %bitcast.16, f32[128,8192]{1,0:T(8,128)} %bitcast.17), custom_call_target="tpu_custom_call" | custom-call | tf_op jit(solution)/shard_map/pallas_call | solution.py:208
  205.0 0.5 slice.3
  205.5 0.0 copy-done.2
  205.5 0.0 copy-start.1
  205.5 5.2 %fusion.2 = f32[1,128,8192]{2,1,0:T(8,128)} fusion(f32[1,128,8192]{2,1,0:T(8,128)S(1)} %copy-done.2, f32[128,8192]{1,0:T(8,128)} %get-tuple-element.4), kind=kLoop, calls=%fused_computation.4 | loop fusion | flops 5242880 | bytes 12582912 | tf_op jit(solution)/shard_map/broadcast_in_dim | solution.py:244
  210.7 0.0 copy-done.1
  210.7 3.3 %multiply_add_fusion = f32[1,128,8192]{2,1,0:T(8,128)} fusion(bf16[1,128,8192]{2,1,0:T(8,128)(2,1)S(1)} %copy-done, f32[1,128,8192]{2,1,0:T(8,128)S(1)} %copy-done.1, f32[]{:T(128)} %bitcast.4), kind=kLoop, calls=%fused_computation.5 | loop fusion | flops 4194304 | bytes 10485764 | tf_op jit(solution)/shard_map/add | solution.py:241
Async XLA Ops:
  0.6 1.6 copy-start
  2.2 203.3 %copy-start.2 = (f32[1,128,8192]{2,1,0:T(8,128)S(1)}, f32[1,128,8192]{2,1,0:T(8,128)}, u32[]{:S(2)}) copy-start(f32[1,128,8192]{2,1,0:T(8,128)} %param.5) | copy-start | bytes 12582916
  205.5 5.2 %copy-start.1 = (f32[1,128,8192]{2,1,0:T(8,128)S(1)}, f32[1,128,8192]{2,1,0:T(8,128)}, u32[]{:S(2)}) copy-start(f32[1,128,8192]{2,1,0:T(8,128)} %param.4) | copy-start | bytes 12582916

commit v2 on v1

--- a/solution.py
+++ b/solution.py
@@ -48,18 +48,32 @@
     return q / norm
 
 
+def pack(x):
+    half = HD // 2
+    return jnp.stack([x[:half, :half], x[:half, half:], x[half:, half:]])
+
+
+def unpack(x):
+    top = jnp.concatenate([x[0], x[1]], axis=1)
+    return jnp.concatenate([top, jnp.concatenate([x[1].T, x[2]], axis=1)], axis=0)
+
+
 def exchange_kernel(
-    devices, layers, limit, g_ref, m_ref, ret_ref, fac_ref,
-    squares, mine, outgoing, held, result,
-    square_send, square_recv, out_send, out_recv, back_send, back_recv, own_sem,
+    plane, devices, layers, limit, g_ref, m_ref, ret_ref, fac_ref,
+    squares, mine, outgoing, held, result, gram_out, grams, own_q, qs,
+    square_send, square_recv, out_send, out_recv, back_send, back_recv,
+    gram_send, gram_recv, q_send, q_recv, own_sem,
 ):
     rows = g_ref.shape[0]
     heads = g_ref.shape[1] // HD
+    depth = devices // plane
     per_device = heads // devices
+    per_plane = heads // plane
     everyone = devices * layers
     me = lax.axis_index("rows")
     layer = lax.axis_index("layer")
     flat = me * layers + layer
+    z, p = me // plane, me % plane
 
     barrier = pltpu.get_barrier_semaphore()
 
@@ -105,93 +119,168 @@
     factor = jnp.minimum(1.0, limit / (jnp.sqrt(total) + 1e-06))
     fac_ref[...] = jnp.broadcast_to(factor, fac_ref.shape)
 
+    def columns_of(h):
+        return pl.ds(pl.multiple_of(h * HD, HD), HD)
+
     def update_of(h):
-        columns = pl.ds(pl.multiple_of(h * HD, HD), HD)
-        clipped = factor * g_ref[:, columns].astype(jnp.float32)
-        new_momentum = momentum_decay * m_ref[:, columns] + clipped
+        clipped = factor * g_ref[:, columns_of(h)].astype(jnp.float32)
+        new_momentum = momentum_decay * m_ref[:, columns_of(h)] + clipped
         return clipped + momentum_decay * new_momentum
 
     def block(d):
         return pl.ds(pl.multiple_of(d * rows, rows), rows)
 
-    def out_copy(j, k):
-        d = (me + k) % devices
-        return pltpu.make_async_remote_copy(
-            src_ref=outgoing.at[d * per_device + j],
-            dst_ref=held.at[j, block(me)],
-            send_sem=out_send.at[j, k],
-            recv_sem=out_recv.at[j, k],
-            device_id={"rows": d},
-            device_id_type=MESH,
-        )
-
-    def back_copy(j, k):
-        d = (me + k) % devices
-        head = me * per_device + j
-        return pltpu.make_async_remote_copy(
-            src_ref=result.at[j, block(d)],
-            dst_ref=ret_ref.at[:, pl.ds(pl.multiple_of(head * HD, HD), HD)],
-            send_sem=back_send.at[j, k],
-            recv_sem=back_recv.at[j, k],
-            device_id={"rows": d},
-            device_id_type=MESH,
-        )
-
-    def own_copy(j):
-        head = me * per_device + j
+    def chunk(j, kz):
+        return j * depth + (z + kz) % depth
+
+    def out_copy(j, kz, kp):
+        d = (p + kp) % plane
+        c = chunk(j, kz)
+        return pltpu.make_async_remote_copy(
+            src_ref=outgoing.at[d * per_plane + c],
+            dst_ref=held.at[c, block(p)],
+            send_sem=out_send.at[j, kz, kp],
+            recv_sem=out_recv.at[j, kz, kp],
+            device_id={"rows": z * plane + d},
+            device_id_type=MESH,
+        )
+
+    def back_copy(j, kz, kp):
+        d = (p + kp) % plane
+        c = chunk(j, kz)
+        return pltpu.make_async_remote_copy(
+            src_ref=result.at[c, block(d)],
+            dst_ref=ret_ref.at[:, columns_of(p * per_plane + c)],
+            send_sem=back_send.at[j, kz, kp],
+            recv_sem=back_recv.at[j, kz, kp],
+            device_id={"rows": z * plane + d},
+            device_id_type=MESH,
+        )
+
+    def own_copy(j, kz):
+        c = chunk(j, kz)
         return pltpu.make_async_copy(
-            result.at[j, block(me)], ret_ref.at[:, pl.ds(pl.multiple_of(head * HD, HD), HD)], own_sem.at[j]
-        )
+            result.at[c, block(p)], ret_ref.at[:, columns_of(p * per_plane + c)], own_sem.at[j, kz]
+        )
+
+    def gram_copy(j, kz):
+        return pltpu.make_async_remote_copy(
+            src_ref=gram_out.at[chunk(j, kz)],
+            dst_ref=grams.at[j, z],
+            send_sem=gram_send.at[j, kz],
+            recv_sem=gram_recv.at[j, kz],
+            device_id={"rows": (z + kz) % depth * plane + p},
+            device_id_type=MESH,
+        )
+
+    def q_copy(j, kz):
+        return pltpu.make_async_remote_copy(
+            src_ref=own_q.at[j],
+            dst_ref=qs.at[j, z],
+            send_sem=q_send.at[j, kz],
+            recv_sem=q_recv.at[j, kz],
+            device_id={"rows": (z + kz) % depth * plane + p},
+            device_id_type=MESH,
+        )
+
+    def send_update(j):
+        @pl.loop(0, depth)
+        def _(i):
+            kz = (i + 1) % depth
+            c = chunk(j, kz)
+
+            @pl.loop(1, plane)
+            def _(kp):
+                h = (p + kp) % plane * per_plane + c
+                outgoing[h] = update_of(h)
+                out_copy(j, kz, kp).start()
+
+            held[c, block(p), :] = update_of(p * per_plane + c)
+
+    def send_gram(j):
+        @pl.loop(0, depth)
+        def _(i):
+            kz = (i + 1) % depth
+
+            @pl.loop(1, plane)
+            def _(kp):
+                out_copy(j, kz, kp).wait_recv()
+
+            x = held[chunk(j, kz)]
+            packed = pack(
+                lax.dot_general(
+                    x, x, (((0,), (0,)), ((), ())), precision=HIGHEST, preferred_element_type=jnp.float32
+                )
+            )
+
+            @pl.when(kz != 0)
+            def _():
+                gram_out[chunk(j, kz)] = packed
+                gram_copy(j, kz).start()
+
+            @pl.when(kz == 0)
+            def _():
+                grams[j, z] = packed
+
+    def send_q(j):
+        @pl.loop(1, depth)
+        def _(kz):
+            gram_copy(j, kz).wait_recv()
+
+        packed = pack(polynomial(unpack(jnp.sum(grams[j], axis=0))))
+        own_q[j] = packed
+        qs[j, z] = packed
+
+        @pl.loop(1, depth)
+        def _(kz):
+            q_copy(j, kz).start()
+
+    def send_result(j):
+        @pl.loop(0, depth)
+        def _(i):
+            kz = (depth - i) % depth
+
+            @pl.when(i != 0)
+            def _():
+                q_copy(j, i).wait_recv()
+
+            c = chunk(j, kz)
+            q_high, q_low = split(unpack(qs[j, (z + kz) % depth]))
+            high, low = split(held[c])
+            dot = functools.partial(jnp.dot, preferred_element_type=jnp.float32)
+            result[c] = dot(high, q_high) + (dot(high, q_low) + dot(low, q_high))
+
+            @pl.loop(1, plane)
+            def _(kp):
+                back_copy(j, kz, kp).start()
+
+            own_copy(j, kz).start()
+
+    for j in range(per_device):
+        send_update(j)
+    for j in range(per_device):
+        send_gram(j)
+        if j > 0:
+            send_result(j - 1)
+        send_q(j)
+    send_result(per_device - 1)
 
     @pl.loop(0, per_device)
     def _(j):
-        @pl.loop(1, devices)
-        def _(k):
-            h = (me + k) % devices * per_device + j
-            outgoing[h] = update_of(h)
-            out_copy(j, k).start()
-
-        held[j, block(me), :] = update_of(me * per_device + j)
-
-    @pl.loop(0, per_device)
-    def _(j):
-        @pl.loop(1, devices)
-        def _(k):
-            out_copy(j, k).wait_recv()
-
-        step = 2 * rows
-
-        def add_gram(s, gram):
-            x = held[j, pl.ds(pl.multiple_of(s * step, step), step), :]
-            return gram + lax.dot_general(
-                x, x, (((0,), (0,)), ((), ())), precision=HIGHEST, preferred_element_type=jnp.float32
-            )
-
-        gram = lax.fori_loop(0, devices // 2, add_gram, jnp.zeros((HD, HD), jnp.float32))
-        q_high, q_low = split(polynomial(gram))
-
-        def apply(d):
-            high, low = split(held[j, block(d), :])
-            dot = functools.partial(jnp.dot, preferred_element_type=jnp.float32)
-            result[j, block(d), :] = dot(high, q_high) + (dot(high, q_low) + dot(low, q_high))
-
-        @pl.loop(1, devices)
-        def _(k):
-            apply((me + k) % devices)
-            back_copy(j, k).start()
-
-        apply(me)
-        own_copy(j).start()
-
-    @pl.loop(0, per_device)
-    def _(j):
-        own_copy(j).wait()
-
-        @pl.loop(1, devices)
-        def _(k):
-            back_copy(j, k).wait_recv()
-            back_copy(j, k).wait_send()
-            out_copy(j, k).wait_send()
+        @pl.loop(0, depth)
+        def _(kz):
+            own_copy(j, kz).wait()
+
+            @pl.loop(1, plane)
+            def _(kp):
+                back_copy(j, kz, kp).wait_recv()
+                back_copy(j, kz, kp).wait_send()
+                out_copy(j, kz, kp).wait_send()
+
+        @pl.loop(1, depth)
+        def _(kz):
+            gram_copy(j, kz).wait_send()
+            q_copy(j, kz).wait_send()
 
     @pl.loop(1, everyone)
     def _(k):
@@ -201,12 +290,16 @@
 def exchange(gradient, momentum, devices, layers, limit):
     rows, width = gradient.shape
     heads = width // HD
+    plane = math.gcd(devices, 1 << (devices.bit_length() // 2))
+    depth = devices // plane
     per_device = heads // devices
+    per_plane = heads // plane
     everyone = devices * layers
-    latent = rows * devices
     dma = pltpu.SemaphoreType.DMA
+    vmem = lambda *shape: pltpu.VMEM(shape, jnp.float32)
+    packed = (3, HD // 2, HD // 2)
     return pl.pallas_call(
-        functools.partial(exchange_kernel, devices, layers, limit),
+        functools.partial(exchange_kernel, plane, devices, layers, limit),
         out_shape=(
             jax.ShapeDtypeStruct((rows, width), jnp.float32),
             jax.ShapeDtypeStruct((8, 128), jnp.float32),
@@ -214,18 +307,26 @@
         in_specs=[pl.BlockSpec(memory_space=pltpu.VMEM)] * 2,
         out_specs=(pl.BlockSpec(memory_space=pl.ANY), pl.BlockSpec(memory_space=pltpu.VMEM)),
         scratch_shapes=[
-            pltpu.VMEM((everyone, 8, 128), jnp.float32),
-            pltpu.VMEM((8, 128), jnp.float32),
-            pltpu.VMEM((heads, rows, HD), jnp.float32),
-            pltpu.VMEM((per_device, latent, HD), jnp.float32),
-            pltpu.VMEM((per_device, latent, HD), jnp.float32),
+            vmem(everyone, 8, 128),
+            vmem(8, 128),
+            vmem(heads, rows, HD),
+            vmem(per_plane, plane * rows, HD),
+            vmem(per_plane, plane * rows, HD),
+            vmem(per_plane, *packed),
+            vmem(per_device, depth, *packed),
+            vmem(per_device, *packed),
+            vmem(per_device, depth, *packed),
             dma((everyone,)),
             dma((everyone,)),
-            dma((per_device, devices)),
-            dma((per_device, devices)),
-            dma((per_device, devices)),
-            dma((per_device, devices)),
-            dma((per_device,)),
+            dma((per_device, depth, plane)),
+            dma((per_device, depth, plane)),
+            dma((per_device, depth, plane)),
+            dma((per_device, depth, plane)),
+            dma((per_device, depth)),
+            dma((per_device, depth)),
+            dma((per_device, depth)),
+            dma((per_device, depth)),
+            dma((per_device, depth)),
         ],
         compiler_params=pltpu.CompilerParams(
             collective_id=0, has_side_effects=True, vmem_limit_bytes=48 * 1024 * 1024

time: 214 us -> 131 us (0.61)
  the two profiles are of different devices: /device:TPU:14 before, /device:TPU:16 now
where the time goes in v2:
time: 131 us
  Pallas kernels  120 us (92%)
  other arithmetic  8.48 us (6%)
  local copies, waits for them, and re-layouts  2.1 us (2%)
    pallas_call x1, Pallas kernels, exchange(): pl.pallas_call(functools.partial(exchange_kernel, plane, devices, layers,...  120 us
    broadcast_in_dim x1, other arithmetic, body(): return (new_weights[None], new_momentum[None])  5.22 us
    add x1, other arithmetic, body(): momentum_decay * momentum[0] + fac[0, 0] * grads[0].astype(jnp.float32)  3.26 us

profile of v2, /device:TPU:16, one launch (start us, length us, event | category | flops | bytes accessed | tf_op | source)
XLA Modules:
  0.0 130.9 jit_solution(9170449216007326712)
XLA Ops:
  0.6 0.0 copy-start
  0.6 1.6 %copy-done = bf16[1,128,8192]{2,1,0:T(8,128)(2,1)S(1)} copy-done((bf16[1,128,8192]{2,1,0:T(8,128)(2,1)S(1)}, bf16[1,128,8192]{2,1,0:T(8,128)(2,1)}, u32[]{:S(2)}) %copy-start) | copy-done | bytes 2097176
  2.2 0.0 copy-start.2
  2.2 119.7 %shard_map.50 = (f32[128,8192]{1,0:T(8,128)}, f32[8,128]{1,0:T(8,128)S(1)}) custom-call(bf16[128,8192]{1,0:T(8,128)(2,1)S(1)} %bitcast.16, f32[128,8192]{1,0:T(8,128)} %bitcast.17), custom_call_target="tpu_custom_call" | custom-call | tf_op jit(solution)/shard_map/pallas_call | solution.py:301
  122.0 0.5 slice.3
  122.5 0.0 copy-done.2
  122.5 0.0 copy-start.1
  122.5 5.2 %fusion.2 = f32[1,128,8192]{2,1,0:T(8,128)} fusion(f32[1,128,8192]{2,1,0:T(8,128)S(1)} %copy-done.2, f32[128,8192]{1,0:T(8,128)} %get-tuple-element.4), kind=kLoop, calls=%fused_computation.4 | loop fusion | flops 5242880 | bytes 12582912 | tf_op jit(solution)/shard_map/broadcast_in_dim | solution.py:345
  127.7 0.0 copy-done.1
  127.7 3.3 %multiply_add_fusion = f32[1,128,8192]{2,1,0:T(8,128)} fusion(bf16[1,128,8192]{2,1,0:T(8,128)(2,1)S(1)} %copy-done, f32[1,128,8192]{2,1,0:T(8,128)S(1)} %copy-done.1, f32[]{:T(128)} %bitcast.4), kind=kLoop, calls=%fused_computation.5 | loop fusion | flops 4194304 | bytes 10485764 | tf_op jit(solution)/shard_map/add | solution.py:342
Async XLA Ops:
  0.6 1.6 %copy-start = (bf16[1,128,8192]{2,1,0:T(8,128)(2,1)S(1)}, bf16[1,128,8192]{2,1,0:T(8,128)(2,1)}, u32[]{:S(2)}) copy-start(bf16[1,128,8192]{2,1,0:T(8,128)(2,1)} %param.3) | copy-start | bytes 6291460
  2.2 120.2 %copy-start.2 = (f32[1,128,8192]{2,1,0:T(8,128)S(1)}, f32[1,128,8192]{2,1,0:T(8,128)}, u32[]{:S(2)}) copy-start(f32[1,128,8192]{2,1,0:T(8,128)} %param.5) | copy-start | bytes 12582916
  122.5 5.2 %copy-start.1 = (f32[1,128,8192]{2,1,0:T(8,128)S(1)}, f32[1,128,8192]{2,1,0:T(8,128)}, u32[]{:S(2)}) copy-start(f32[1,128,8192]{2,1,0:T(8,128)} %param.4) | copy-start | bytes 12582916

commit v3 on v2

--- a/solution.py
+++ b/solution.py
@@ -59,10 +59,10 @@
 
 
 def exchange_kernel(
-    plane, devices, layers, limit, g_ref, m_ref, ret_ref, fac_ref,
-    squares, mine, outgoing, held, result, gram_out, grams, own_q, qs,
+    plane, devices, layers, limit, scale, g_ref, m_hbm, w_hbm, new_w_ref, new_m_ref,
+    m_ref, w_ref, returned, squares, mine, outgoing, held, result, gram_out, grams, own_q, qs,
     square_send, square_recv, out_send, out_recv, back_send, back_recv,
-    gram_send, gram_recv, q_send, q_recv, own_sem,
+    gram_send, gram_recv, q_send, q_recv, load_sem,
 ):
     rows = g_ref.shape[0]
     heads = g_ref.shape[1] // HD
@@ -75,6 +75,10 @@
     flat = me * layers + layer
     z, p = me // plane, me % plane
 
+    load_m = pltpu.make_async_copy(m_hbm, m_ref, load_sem.at[0])
+    load_w = pltpu.make_async_copy(w_hbm, w_ref, load_sem.at[1])
+    load_m.start()
+    load_w.start()
     barrier = pltpu.get_barrier_semaphore()
 
     @pl.loop(1, everyone)
@@ -117,7 +121,8 @@
     total = jnp.sum(squares[...], axis=0)
     total = jnp.sum(jnp.sum(total, axis=0, keepdims=True), axis=1, keepdims=True)
     factor = jnp.minimum(1.0, limit / (jnp.sqrt(total) + 1e-06))
-    fac_ref[...] = jnp.broadcast_to(factor, fac_ref.shape)
+    load_m.wait()
+    load_w.wait()
 
     def columns_of(h):
         return pl.ds(pl.multiple_of(h * HD, HD), HD)
@@ -125,6 +130,7 @@
     def update_of(h):
         clipped = factor * g_ref[:, columns_of(h)].astype(jnp.float32)
         new_momentum = momentum_decay * m_ref[:, columns_of(h)] + clipped
+        new_m_ref[:, columns_of(h)] = new_momentum
         return clipped + momentum_decay * new_momentum
 
     def block(d):
@@ -150,18 +156,16 @@
         c = chunk(j, kz)
         return pltpu.make_async_remote_copy(
             src_ref=result.at[c, block(d)],
-            dst_ref=ret_ref.at[:, columns_of(p * per_plane + c)],
+            dst_ref=returned.at[p * per_plane + c],
             send_sem=back_send.at[j, kz, kp],
             recv_sem=back_recv.at[j, kz, kp],
             device_id={"rows": z * plane + d},
             device_id_type=MESH,
         )
 
-    def own_copy(j, kz):
-        c = chunk(j, kz)
-        return pltpu.make_async_copy(
-            result.at[c, block(p)], ret_ref.at[:, columns_of(p * per_plane + c)], own_sem.at[j, kz]
-        )
+    def finish(h, ortho):
+        w = w_ref[:, columns_of(h)]
+        new_w_ref[:, columns_of(h)] = w - learn_rate * (scale * ortho + weight_decay * w)
 
     def gram_copy(j, kz):
         return pltpu.make_async_remote_copy(
@@ -254,7 +258,7 @@
             def _(kp):
                 back_copy(j, kz, kp).start()
 
-            own_copy(j, kz).start()
+            finish(p * per_plane + c, result[c, block(p), :])
 
     for j in range(per_device):
         send_update(j)
@@ -268,12 +272,21 @@
     @pl.loop(0, per_device)
     def _(j):
         @pl.loop(0, depth)
-        def _(kz):
-            own_copy(j, kz).wait()
+        def _(i):
+            kz = (depth - i) % depth
 
             @pl.loop(1, plane)
             def _(kp):
                 back_copy(j, kz, kp).wait_recv()
+                h = (p + plane - kp) % plane * per_plane + chunk(j, kz)
+                finish(h, returned[h])
+
+    @pl.loop(0, per_device)
+    def _(j):
+        @pl.loop(0, depth)
+        def _(kz):
+            @pl.loop(1, plane)
+            def _(kp):
                 back_copy(j, kz, kp).wait_send()
                 out_copy(j, kz, kp).wait_send()
 
@@ -287,7 +300,7 @@
         square_copy(k).wait_send()
 
 
-def exchange(gradient, momentum, devices, layers, limit):
+def exchange(gradient, momentum, weights, devices, layers, limit, scale):
     rows, width = gradient.shape
     heads = width // HD
     plane = math.gcd(devices, 1 << (devices.bit_length() // 2))
@@ -299,14 +312,17 @@
     vmem = lambda *shape: pltpu.VMEM(shape, jnp.float32)
     packed = (3, HD // 2, HD // 2)
     return pl.pallas_call(
-        functools.partial(exchange_kernel, plane, devices, layers, limit),
+        functools.partial(exchange_kernel, plane, devices, layers, limit, scale),
         out_shape=(
             jax.ShapeDtypeStruct((rows, width), jnp.float32),
-            jax.ShapeDtypeStruct((8, 128), jnp.float32),
+            jax.ShapeDtypeStruct((rows, width), jnp.float32),
         ),
-        in_specs=[pl.BlockSpec(memory_space=pltpu.VMEM)] * 2,
-        out_specs=(pl.BlockSpec(memory_space=pl.ANY), pl.BlockSpec(memory_space=pltpu.VMEM)),
+        in_specs=[pl.BlockSpec(memory_space=pltpu.VMEM)] + [pl.BlockSpec(memory_space=pl.ANY)] * 2,
+        out_specs=(pl.BlockSpec(memory_space=pltpu.VMEM), pl.BlockSpec(memory_space=pltpu.VMEM)),
         scratch_shapes=[
+            vmem(rows, width),
+            vmem(rows, width),
+            vmem(heads, rows, HD),
             vmem(everyone, 8, 128),
             vmem(8, 128),
             vmem(heads, rows, HD),
@@ -326,22 +342,20 @@
             dma((per_device, depth)),
             dma((per_device, depth)),
             dma((per_device, depth)),
-            dma((per_device, depth)),
+            dma((2,)),
         ],
         compiler_params=pltpu.CompilerParams(
-            collective_id=0, has_side_effects=True, vmem_limit_bytes=48 * 1024 * 1024
+            collective_id=0, has_side_effects=True, vmem_limit_bytes=40 * 1024 * 1024
         ),
-    )(gradient, momentum)
+    )(gradient, momentum, weights)
 
 
 def body(grads, momentum, weights):
     devices, layers = lax.axis_size("rows"), lax.axis_size("layer")
     rows, width = grads.shape[1:]
     limit = 0.5 * math.sqrt(float(layers * devices * rows * width))
-    returned, fac = exchange(grads[0], momentum[0], devices, layers, limit)
-    new_momentum = momentum_decay * momentum[0] + fac[0, 0] * grads[0].astype(jnp.float32)
     scale = 0.2 * math.sqrt(float(max(devices * rows, HD)))
-    new_weights = weights[0] - learn_rate * (scale * returned + weight_decay * weights[0])
+    new_weights, new_momentum = exchange(grads[0], momentum[0], weights[0], devices, layers, limit, scale)
     return (new_weights[None], new_momentum[None])
 
 

time: 131 us -> 124 us (0.947)
  other arithmetic: 8.48 us -> 0 us
  local copies, waits for them, and re-layouts: 2.1 us -> 5.61 us
  Pallas kernels: 120 us -> 117 us
    broadcast_in_dim x1 -> x0, other arithmetic: 5.22 us -> none  [body(): return (new_weights[None], new_momentum[None])]
    unnamed x6 -> x4, local copies, waits for them, and re-layouts: 1.59 us -> 5.61 us
    add x1 -> x0, other arithmetic: 3.26 us -> none  [body(): momentum_decay * momentum[0] + fac[0, 0] * grads[0].astype(jnp.float32)]
    pallas_call x1, Pallas kernels: 120 us -> 117 us  [exchange(): pl.pallas_call(functools.partial(exchange_kernel, plane, devices, layers,...]
where the time goes in v3:
time: 124 us
  Pallas kernels  117 us (94%)
  local copies, waits for them, and re-layouts  5.61 us (5%)
    pallas_call x1, Pallas kernels, exchange(): pl.pallas_call(functools.partial(exchange_kernel, plane, devices, layers,...  117 us
    unnamed x4, local copies, waits for them, and re-layouts  5.61 us

profile of v3, /device:TPU:16, one launch (start us, length us, event | category | flops | bytes accessed | tf_op | source)
XLA Modules:
  0.0 123.7 jit_solution(11376299701919639699)
XLA Ops:
  0.6 0.0 copy-start
  0.6 1.6 %copy-done = bf16[1,128,8192]{2,1,0:T(8,128)(2,1)S(1)} copy-done((bf16[1,128,8192]{2,1,0:T(8,128)(2,1)S(1)}, bf16[1,128,8192]{2,1,0:T(8,128)(2,1)}, u32[]{:S(2)}) %copy-start) | copy-done | bytes 2097176
  2.2 117.4 %shard_map.50 = (f32[128,8192]{1,0:T(8,128)S(1)}, f32[128,8192]{1,0:T(8,128)S(1)}) custom-call(bf16[128,8192]{1,0:T(8,128)(2,1)S(1)} %bitcast.7, f32[128,8192]{1,0:T(8,128)} %bitcast.8, f32[128,8192]{1,0:T(8,128)} %bitcast.9), custom_call_target="tpu_custom_call" | custom-call | tf_op jit(solution)/shard_map/pallas_call | solution.py:314
  119.6 2.0 %copy.7 = f32[1,128,8192]{2,1,0:T(8,128)} copy(f32[1,128,8192]{2,1,0:T(8,128)S(1)} %bitcast.6) | data formatting | bytes 8388608
  121.6 2.0 %copy.8 = f32[1,128,8192]{2,1,0:T(8,128)} copy(f32[1,128,8192]{2,1,0:T(8,128)S(1)} %bitcast.5) | data formatting | bytes 8388608
Async XLA Ops:
  0.6 1.6 %copy-start = (bf16[1,128,8192]{2,1,0:T(8,128)(2,1)S(1)}, bf16[1,128,8192]{2,1,0:T(8,128)(2,1)}, u32[]{:S(2)}) copy-start(bf16[1,128,8192]{2,1,0:T(8,128)(2,1)} %param.3) | copy-start | bytes 6291460
